TPU v7x, 32 devices: a whole 2x2x4 slice. The times are simulated.
32 devices in a mesh: leaf: 16 (over z, y, core), top: 2 (over x).
Axes of the slice: x: 2, y: 2, z: 4, core: 2. Of those that a mesh axis runs over, the one named last changes fastest.
Arguments:
- vectors: bfloat16 [2, 16, 768, 512], P('top', 'leaf'), may hold values from -6 to 6
- near_tiles: bfloat16 [2, 16, 8, 768, 768], P('top', 'leaf'), may hold values from -0.078125 to 0.078125
- leaf_basis: bfloat16 [2, 16, 768, 128], P('top', 'leaf'), may hold values from -0.21875 to 0.21875
- transfer: bfloat16 [2, 16, 128, 128], P('top', 'leaf'), may hold values from -0.25 to 0.25
- coupling: bfloat16 [2, 16, 7, 128, 128], P('top', 'leaf'), may hold values from -0.1875 to 0.1875
- top_coupling: bfloat16 [2, 2, 128, 128], P('top'), may hold values from -0.375 to 0.375
- near_list: int32 [2, 16, 8], P('top', 'leaf'), may hold values from -4 to 4, as said below
- far_list: int32 [2, 16, 7], P('top', 'leaf'), may hold values from 0 to 15, as said below
- row_counts: int32 [2, 16], P('top', 'leaf'), may hold values from 384 to 768
Outputs:
- product: float32 [2, 16, 768, 512], P('top', 'leaf')
Inputs may be any that keep to these rules, and one draw needn't show every extreme that they name: `near_list`: each leaf's 8 offsets are distinct; an offset that leads outside the cluster's 16 leaves stands for an absent block. `far_list`: each leaf's entries are distinct positions in its cluster, each more than 4 away from the leaf's own position. `row_counts`: rows at and beyond the count are padding.
All inputs are finite; a program needn't handle non-finite values.
Results may differ from a plain program's by a relative error of at most 0.0045.
Values may be sent and summed in bfloat16 or wider, within the bound.
A program may use at most 128 MiB of HBM per device.

v0:
```python
import jax
import jax.numpy as jnp
from jax import lax
from jax.sharding import PartitionSpec as P

REACH = 4


def passed_along(block, axis, distance):
    devices = range(lax.axis_size(axis))
    route = [(i - distance, i) for i in devices if i - distance in devices]
    return lax.ppermute(block, axis, route)


def body(
    vectors,
    near_tiles,
    leaf_basis,
    transfer,
    coupling,
    top_coupling,
    near_list,
    far_list,
    row_counts,
):
    leaf_rows = vectors.shape[2]
    row_index = jnp.arange(leaf_rows, dtype=jnp.int32)
    keep = (row_index < row_counts[0, 0]).astype(jnp.bfloat16)
    masked = vectors[0, 0] * keep[:, None]
    offsets = near_list[0, 0]
    tiles = near_tiles[0, 0]
    window = []
    for offset in range(-REACH, REACH + 1):
        if offset == 0:
            window.append(masked)
        else:
            window.append(passed_along(masked, "leaf", -offset))
    stacked = jnp.stack(window)
    span = jnp.arange(-REACH, REACH + 1, dtype=jnp.int32)
    picker = (offsets[:, None] == span[None, :]).astype(jnp.bfloat16)
    sources = jnp.einsum("kw,wrv->krv", picker, stacked, preferred_element_type=jnp.float32)
    near = jnp.einsum(
        "kij,kjv->iv", tiles, sources.astype(jnp.bfloat16), preferred_element_type=jnp.float32
    )
    basis = leaf_basis[0, 0]
    coeff = jnp.einsum("ir,iv->rv", basis, masked, preferred_element_type=jnp.float32).astype(
        jnp.bfloat16
    )
    nested = transfer[0, 0]
    upward = jnp.einsum("ab,av->bv", nested, coeff, preferred_element_type=jnp.float32)
    clusters = lax.axis_size("top")
    owner = (jnp.arange(clusters, dtype=jnp.int32) == lax.axis_index("top")).astype(jnp.float32)
    parents = lax.psum(owner[:, None, None] * upward[None], ("leaf", "top")).astype(jnp.bfloat16)
    sibling_ids = (lax.axis_index("top") + 1 + jnp.arange(clusters, dtype=jnp.int32)) % clusters
    top_pick = (sibling_ids[:, None] == jnp.arange(clusters, dtype=jnp.int32)[None, :]).astype(
        jnp.bfloat16
    )
    chosen = jnp.einsum(
        "mc,crv->mrv", top_pick, parents, preferred_element_type=jnp.float32
    ).astype(jnp.bfloat16)
    parent_field = jnp.einsum(
        "mab,mbv->av", top_coupling[0], chosen, preferred_element_type=jnp.float32
    ).astype(jnp.bfloat16)
    siblings = far_list[0, 0]
    matrices = coupling[0, 0]
    piece = lax.all_gather(coeff[None], "leaf", axis=0, tiled=True)
    blocks = jnp.arange(piece.shape[0], dtype=jnp.int32)
    chooser = (siblings[:, None] == blocks[None, :]).astype(jnp.bfloat16)
    gathered = jnp.einsum("mn,nrv->mrv", chooser, piece, preferred_element_type=jnp.float32).astype(
        jnp.bfloat16
    )
    local_field = jnp.einsum("mab,mbv->av", matrices, gathered, preferred_element_type=jnp.float32)
    local_field = (
        local_field + jnp.dot(nested, parent_field, preferred_element_type=jnp.float32)
    ).astype(jnp.bfloat16)
    result = near + jnp.dot(basis, local_field, preferred_element_type=jnp.float32)
    result = result * keep[:, None].astype(jnp.float32)
    return result[None, None]


def solution(mesh):
    in_specs = (
        P("top", "leaf", None, None),
        P("top", "leaf", None, None, None),
        P("top", "leaf", None, None),
        P("top", "leaf", None, None),
        P("top", "leaf", None, None, None),
        P("top", None, None, None),
        P("top", "leaf", None),
        P("top", "leaf", None),
        P("top", "leaf"),
    )
    out_specs = P("top", "leaf", None, None)
    return jax.shard_map(body, mesh=mesh, in_specs=in_specs, out_specs=out_specs, check_vma=False)
```

profile of v0, /device:TPU:0, one launch (start us, length us, event | category | flops | bytes accessed | tf_op | source)
XLA Modules:
  0.0 217.3 jit_solution(1711316566224805380)
XLA Ops:
  7.3 1.3 bitcast_multiply_fusion.1
  8.6 5.9 %collective-permute-start = (bf16[768,512]{1,0:T(8,128)(2,1)S(1)}, bf16[768,512]{1,0:T(8,128)(2,1)}, u32[]{:S(2)}, u32[]{:S(2)}) collective-permute-start(bf16[768,512]{1,0:T(8,128)(2,1)S(1)} %bitcast_multiply_fusion.1), channel_id=1, source_target_pairs={{0,8},{2,10},{4,12},{6,14},{8,16},{10,18},{12,20},{14,22},{16,24},... | collective-permute-start | bytes 2359304 | tf_op jit(solution)/shard_map/ppermute | solution.py:12
  14.5 3.5 %collective-permute-start.1 = (bf16[768,512]{1,0:T(8,128)(2,1)S(1)}, bf16[768,512]{1,0:T(8,128)(2,1)}, u32[]{:S(2)}, u32[]{:S(2)}) collective-permute-start(bf16[768,512]{1,0:T(8,128)(2,1)S(1)} %bitcast_multiply_fusion.1), channel_id=1, source_target_pairs={{0,6},{2,8},{4,10},{6,12},{8,14},{10,16},{12,18},{14,20},{16,22},{... | collective-permute-start | bytes 2359304 | tf_op jit(solution)/shard_map/ppermute | solution.py:12
  18.0 3.4 %collective-permute-start.2 = (bf16[768,512]{1,0:T(8,128)(2,1)S(1)}, bf16[768,512]{1,0:T(8,128)(2,1)}, u32[]{:S(2)}, u32[]{:S(2)}) collective-permute-start(bf16[768,512]{1,0:T(8,128)(2,1)S(1)} %bitcast_multiply_fusion.1), channel_id=1, source_target_pairs={{0,4},{2,6},{4,8},{6,10},{8,12},{10,14},{12,16},{14,18},{16,20},{1... | collective-permute-start | bytes 2359304 | tf_op jit(solution)/shard_map/ppermute | solution.py:12
  21.4 2.6 %collective-permute-start.3 = (bf16[768,512]{1,0:T(8,128)(2,1)S(1)}, bf16[768,512]{1,0:T(8,128)(2,1)}, u32[]{:S(2)}, u32[]{:S(2)}) collective-permute-start(bf16[768,512]{1,0:T(8,128)(2,1)S(1)} %bitcast_multiply_fusion.1), channel_id=1, source_target_pairs={{0,2},{2,4},{4,6},{6,8},{8,10},{10,12},{12,14},{14,16},{16,18},{18... | collective-permute-start | bytes 2359304 | tf_op jit(solution)/shard_map/ppermute | solution.py:12
  24.0 1.3 collective-permute-start.4
  25.3 2.4 %convolution_convert_fusion = bf16[512,128]{1,0:T(8,128)(2,1)} fusion(bf16[1,1,768,512]{3,2,1,0:T(8,128)(2,1)} %param.9, bf16[768]{0:T(1024)(128)(2,1)S(1)} %fusion.27, bf16[1,1,768,128]{3,2,1,0:T(8,128)(2,1)} %param.11), kind=kOutput, calls=%fused_computation.15 | convolution fusion | flops 101122048 | bytes 1115648 | tf_op jit(solution)/shard_map/ir,iv->rv/dot_general | solution.py:46
  27.7 1.1 convolution_bitcast_fusion.1
  28.9 0.1 broadcast_multiply_fusion
  29.0 86.0 %all-reduce.1 = bf16[2,128,512]{2,1,0:T(8,128)(2,1)S(1)} all-reduce(f32[2,128,512]{2,1,0:T(8,128)S(1)} %broadcast_multiply_fusion), channel_id=1, replica_groups=mesh['leaf'=16,'top'=2] {'leaf','top'}, use_global_device_ids=true, to_apply=%region_0.0 | all-reduce | flops 131072 | bytes 786432 | tf_op jit(solution)/shard_map/psum | solution.py:53
  115.0 0.5 fusion.18
  115.5 1.1 fusion.11
  116.6 1.3 collective-permute-start.5
  117.9 1.2 bitcast_dynamic-update-slice_fusion.7
  119.1 1.3 collective-permute-start.6
  120.4 1.2 bitcast_dynamic-update-slice_fusion.6
  121.6 1.5 collective-permute-start.7
  123.1 1.2 bitcast_dynamic-update-slice_fusion.5
  124.3 1.2 bitcast_dynamic-update-slice_fusion.4
  125.5 0.2 fusion.15
  125.8 13.1 %collective-permute-done.5 = bf16[768,512]{1,0:T(8,128)(2,1)S(1)} collective-permute-done((bf16[768,512]{1,0:T(8,128)(2,1)S(1)}, bf16[768,512]{1,0:T(8,128)(2,1)S(1)}, u32[]{:S(2)}, u32[]{:S(2)}) %collective-permute-start.5) | collective-permute-done | bytes 786464 | tf_op jit(solution)/shard_map/ppermute | solution.py:12
  139.0 5.5 %collective-permute-done.6 = bf16[768,512]{1,0:T(8,128)(2,1)S(1)} collective-permute-done((bf16[768,512]{1,0:T(8,128)(2,1)S(1)}, bf16[768,512]{1,0:T(8,128)(2,1)S(1)}, u32[]{:S(2)}, u32[]{:S(2)}) %collective-permute-start.6) | collective-permute-done | bytes 786464 | tf_op jit(solution)/shard_map/ppermute | solution.py:12
  144.5 26.2 %collective-permute-done.7 = bf16[768,512]{1,0:T(8,128)(2,1)S(1)} collective-permute-done((bf16[768,512]{1,0:T(8,128)(2,1)S(1)}, bf16[768,512]{1,0:T(8,128)(2,1)S(1)}, u32[]{:S(2)}, u32[]{:S(2)}) %collective-permute-start.7) | collective-permute-done | bytes 786464 | tf_op jit(solution)/shard_map/ppermute | solution.py:12
  170.8 8.7 %fusion = bf16[8,768,512]{2,0,1:T(8,128)(2,1)} fusion(bf16[9,768,512]{2,1,0:T(8,128)(2,1)S(1)} %bitcast_dynamic-update-slice_fusion, s32[9]{0:T(128)S(1)} %iota_add_fusion, s32[8]{0:T(128)S(1)} %bitcast.91), kind=kOutput, calls=%fused_computation | convolution fusion | flops 56623176 | bytes 13369412 | tf_op jit(solution)/shard_map/kw,wrv->krv/dot_general | solution.py:41
  179.4 9.1 %copy.12 = bf16[8,768,512]{1,2,0:T(8,128)(2,1)} copy(bf16[8,768,512]{2,0,1:T(8,128)(2,1)} %fusion) | data formatting | bytes 12582912 | tf_op jit(solution)/shard_map/kw,wrv->krv/dot_general | solution.py:41
  188.5 2.3 %copy.17 = bf16[64,8,16,128]{3,2,1,0:T(8,128)(2,1)S(1)} copy(bf16[64,8,16,128]{3,1,2,0:T(8,128)(2,1)} %bitcast.89) | data formatting | bytes 4194304
  190.8 3.6 %copy.13 = bf16[16,128,512]{2,0,1:T(8,128)(2,1)} copy(bf16[16,128,512]{1,0,2:T(8,128)(2,1)S(1)} %bitcast.88) | data formatting | bytes 4194304 | tf_op jit(solution)/shard_map/all_gather | solution.py:66
  194.3 2.1 fusion.29
  196.4 0.6 convolution_bitcast_fusion.2
  197.0 1.7 fusion.13
  198.7 10.2 %fusion.6 = f32[1,1,768,512]{2,3,1,0:T(8,128)S(1)} fusion(f32[512,768]{1,0:T(8,128)} %fusion.13, bf16[1,1,8,768,768]{4,3,2,1,0:T(8,128)(2,1)} %param.10, bf16[8,768,512]{1,2,0:T(8,128)(2,1)} %copy.12, f32[768]{0:T(1024)S(1)} %fusion.37), kind=kOutput, calls=%fused_computation.8 | convolution fusion | flops 4832624640 | bytes 18877440 | tf_op jit(solution)/shard_map/kij,kjv->iv/dot_general | solution.py:42
  208.9 1.6 copy.10
  (29 shorter events, 0.3 us)
Async XLA Ops:
  6.5 189.9 %copy-start = (bf16[1,1,7,128,128]{4,3,2,1,0:T(8,128)(2,1)S(1)}, bf16[1,1,7,128,128]{4,3,2,1,0:T(8,128)(2,1)}, u32[]{:S(2)}) copy-start(bf16[1,1,7,128,128]{4,3,2,1,0:T(8,128)(2,1)} %param.13) | copy-start | bytes 688132
  6.5 119.0 %copy-start.1 = (bf16[1,1,768,512]{3,2,1,0:T(8,128)(2,1)S(1)}, bf16[1,1,768,512]{3,2,1,0:T(8,128)(2,1)}, u32[]{:S(2)}) copy-start(bf16[1,1,768,512]{3,2,1,0:T(8,128)(2,1)} %param.9) | copy-start | bytes 2359300
  6.5 182.0 %all-gather.3.cloned.1.call-start = ((), (), s32[]{:S(2)}) async-start(), calls=%async_computation | async-start | bytes 2228224 | tf_op jit(solution)/shard_map/all_gather | solution.py:66
  8.6 108.0 %collective-permute-start = (bf16[768,512]{1,0:T(8,128)(2,1)S(1)}, bf16[768,512]{1,0:T(8,128)(2,1)}, u32[]{:S(2)}, u32[]{:S(2)}) collective-permute-start(bf16[768,512]{1,0:T(8,128)(2,1)S(1)} %bitcast_multiply_fusion.1), channel_id=1, source_target_pairs={{0,8},{2,10},{4,12},{6,14},{8,16},{10,18},{12,20},{14,22},{16,24},... | collective-permute-start | bytes 2359304 | tf_op jit(solution)/shard_map/ppermute | solution.py:12
  14.5 104.7 %collective-permute-start.1 = (bf16[768,512]{1,0:T(8,128)(2,1)S(1)}, bf16[768,512]{1,0:T(8,128)(2,1)}, u32[]{:S(2)}, u32[]{:S(2)}) collective-permute-start(bf16[768,512]{1,0:T(8,128)(2,1)S(1)} %bitcast_multiply_fusion.1), channel_id=1, source_target_pairs={{0,6},{2,8},{4,10},{6,12},{8,14},{10,16},{12,18},{14,20},{16,22},{... | collective-permute-start | bytes 2359304 | tf_op jit(solution)/shard_map/ppermute | solution.py:12
  18.0 103.6 %collective-permute-start.2 = (bf16[768,512]{1,0:T(8,128)(2,1)S(1)}, bf16[768,512]{1,0:T(8,128)(2,1)}, u32[]{:S(2)}, u32[]{:S(2)}) collective-permute-start(bf16[768,512]{1,0:T(8,128)(2,1)S(1)} %bitcast_multiply_fusion.1), channel_id=1, source_target_pairs={{0,4},{2,6},{4,8},{6,10},{8,12},{10,14},{12,16},{14,18},{16,20},{1... | collective-permute-start | bytes 2359304 | tf_op jit(solution)/shard_map/ppermute | solution.py:12
  21.4 102.9 %collective-permute-start.3 = (bf16[768,512]{1,0:T(8,128)(2,1)S(1)}, bf16[768,512]{1,0:T(8,128)(2,1)}, u32[]{:S(2)}, u32[]{:S(2)}) collective-permute-start(bf16[768,512]{1,0:T(8,128)(2,1)S(1)} %bitcast_multiply_fusion.1), channel_id=1, source_target_pairs={{0,2},{2,4},{4,6},{6,8},{8,10},{10,12},{12,14},{14,16},{16,18},{18... | collective-permute-start | bytes 2359304 | tf_op jit(solution)/shard_map/ppermute | solution.py:12
  24.0 101.8 %collective-permute-start.4 = (bf16[768,512]{1,0:T(8,128)(2,1)S(1)}, bf16[768,512]{1,0:T(8,128)(2,1)S(1)}, u32[]{:S(2)}, u32[]{:S(2)}) collective-permute-start(bf16[768,512]{1,0:T(8,128)(2,1)S(1)} %bitcast_multiply_fusion.1), channel_id=1, source_target_pairs={{2,0},{4,2},{6,4},{8,6},{10,8},{12,10},{14,12},{16,14},{18,16},{20... | collective-permute-start | bytes 2359304 | tf_op jit(solution)/shard_map/ppermute | solution.py:12
  116.6 54.1 %copy-start.4 = (s32[1,1,8]{2,1,0:T(1,128)S(1)}, s32[1,1,8]{2,1,0:T(1,128)}, u32[]{:S(2)}) copy-start(s32[1,1,8]{2,1,0:T(1,128)} %param.15) | copy-start | bytes 100
  116.6 22.3 %collective-permute-start.5 = (bf16[768,512]{1,0:T(8,128)(2,1)S(1)}, bf16[768,512]{1,0:T(8,128)(2,1)S(1)}, u32[]{:S(2)}, u32[]{:S(2)}) collective-permute-start(bf16[768,512]{1,0:T(8,128)(2,1)S(1)} %bitcast_multiply_fusion.1), channel_id=1, source_target_pairs={{4,0},{6,2},{8,4},{10,6},{12,8},{14,10},{16,12},{18,14},{20,16},{2... | collective-permute-start | bytes 2359304 | tf_op jit(solution)/shard_map/ppermute | solution.py:12
  119.1 25.3 %collective-permute-start.6 = (bf16[768,512]{1,0:T(8,128)(2,1)S(1)}, bf16[768,512]{1,0:T(8,128)(2,1)S(1)}, u32[]{:S(2)}, u32[]{:S(2)}) collective-permute-start(bf16[768,512]{1,0:T(8,128)(2,1)S(1)} %bitcast_multiply_fusion.1), channel_id=1, source_target_pairs={{6,0},{8,2},{10,4},{12,6},{14,8},{16,10},{18,12},{20,14},{22,16},{... | collective-permute-start | bytes 2359304 | tf_op jit(solution)/shard_map/ppermute | solution.py:12
  121.6 49.1 %collective-permute-start.7 = (bf16[768,512]{1,0:T(8,128)(2,1)S(1)}, bf16[768,512]{1,0:T(8,128)(2,1)S(1)}, u32[]{:S(2)}, u32[]{:S(2)}) collective-permute-start(bf16[768,512]{1,0:T(8,128)(2,1)S(1)} %bitcast_multiply_fusion.1), channel_id=1, source_target_pairs={{8,0},{10,2},{12,4},{14,6},{16,8},{18,10},{20,12},{22,14},{24,16},... | collective-permute-start | bytes 2359304 | tf_op jit(solution)/shard_map/ppermute | solution.py:12
  188.5 5.9 %copy-start.5 = (s32[1,1,7]{2,1,0:T(1,128)S(1)}, s32[1,1,7]{2,1,0:T(1,128)}, u32[]{:S(2)}) copy-start(s32[1,1,7]{2,1,0:T(1,128)} %param.16) | copy-start | bytes 88
  188.5 8.5 %copy-start.2 = (bf16[1,1,768,128]{3,2,1,0:T(8,128)(2,1)S(1)}, bf16[1,1,768,128]{3,2,1,0:T(8,128)(2,1)}, u32[]{:S(2)}) copy-start(bf16[1,1,768,128]{3,2,1,0:T(8,128)(2,1)} %param.11) | copy-start | bytes 589828
  188.5 8.5 %copy-start.3 = (bf16[1,1,128,128]{3,2,1,0:T(8,128)(2,1)S(1)}, bf16[1,1,128,128]{3,2,1,0:T(8,128)(2,1)}, u32[]{:S(2)}) copy-start(bf16[1,1,128,128]{3,2,1,0:T(8,128)(2,1)} %param.12) | copy-start | bytes 98308
Sparse Core Ops, SparseCore 0:
  27.8 49.3 all-gather.2
where the time goes:
time: 218 us; the launch traced here: 217 us
  blocking collectives  86 us (39%)
  waiting for transfers between devices  44.8 us (21%)
  matrix products  28.3 us (13%)
  local copies, waits for them, and re-layouts  21.5 us (10%)
  starting transfers between devices  20.7 us (9%)
  between operations  14.4 us (7%)
    psum x1, blocking collectives, body(): lax.psum(owner[:, None, None] * upward[None], ('leaf', 'top'))  86 us
    ppermute x8, waiting for transfers between devices, passed_along(): return lax.ppermute(block, axis, route)  44.8 us
    ppermute x8, starting transfers between devices, passed_along(): return lax.ppermute(block, axis, route)  20.7 us
    dot_general x1, matrix products, body(): jnp.einsum('kij,kjv->iv', tiles, sources.astype(jnp.bfloat16), preferred_...  10.2 us
    dot_general x1, local copies, waits for them, and re-layouts, body(): jnp.einsum('kw,wrv->krv', picker, stacked, preferred_element_type=jnp.flo...  9.06 us
    dot_general x1, matrix products, body(): jnp.einsum('kw,wrv->krv', picker, stacked, preferred_element_type=jnp.flo...  8.66 us
    unnamed x20, local copies, waits for them, and re-layouts  7.17 us
  transfers between devices with their start and end apart: 9, of which 3 were waited for; matrix products, arithmetic and copies ran while one was open for 13% of the time, Pallas kernels for 0%

commit v1 on v0

--- a/solution.py
+++ b/solution.py
@@ -4,6 +4,11 @@
 from jax.sharding import PartitionSpec as P
 
 REACH = 4
+
+
+def axis_by_axis(value, axis_one, axis_two):
+    inner = lax.psum(value, axis_one)
+    return lax.psum(inner, axis_two)
 
 
 def passed_along(block, axis, distance):
@@ -50,7 +55,7 @@
     upward = jnp.einsum("ab,av->bv", nested, coeff, preferred_element_type=jnp.float32)
     clusters = lax.axis_size("top")
     owner = (jnp.arange(clusters, dtype=jnp.int32) == lax.axis_index("top")).astype(jnp.float32)
-    parents = lax.psum(owner[:, None, None] * upward[None], ("leaf", "top")).astype(jnp.bfloat16)
+    parents = axis_by_axis(owner[:, None, None] * upward[None], "top", "leaf").astype(jnp.bfloat16)
     sibling_ids = (lax.axis_index("top") + 1 + jnp.arange(clusters, dtype=jnp.int32)) % clusters
     top_pick = (sibling_ids[:, None] == jnp.arange(clusters, dtype=jnp.int32)[None, :]).astype(
         jnp.bfloat16

time: 218 us -> 241 us (1.11)
  blocking collectives: 86 us -> 99 us
  waiting for transfers between devices: 44.8 us -> 54.4 us
    psum x0 -> x1, waiting for transfers between devices: none -> 14.2 us  [axis_by_axis(): inner = lax.psum(value, axis_one)]
    psum x1, blocking collectives: 86 us -> 99 us  [axis_by_axis(): return lax.psum(inner, axis_two)]
    ppermute x8, waiting for transfers between devices: 44.8 us -> 40.1 us  [passed_along(): return lax.ppermute(block, axis, route)]
    unnamed x20 -> x22, local copies, waits for them, and re-layouts: 7.17 us -> 6.05 us
  transfers between devices with their start and end apart: 9 -> 10, of which waited for: 3 -> 4; matrix products, arithmetic and copies ran while one was open for 13% -> 11% of each run, Pallas kernels for 0% -> 0%
where the time goes in v1:
time: 241 us; the launch traced here: 240 us
  blocking collectives  99 us (41%)
  waiting for transfers between devices  54.4 us (23%)
  matrix products  28.5 us (12%)
  local copies, waits for them, and re-layouts  20.3 us (8%)
  starting transfers between devices  19.9 us (8%)
  between operations  15.9 us (7%)
  other arithmetic  2.48 us (1%)
    psum x1, blocking collectives, axis_by_axis(): return lax.psum(inner, axis_two)  99 us
    ppermute x8, waiting for transfers between devices, passed_along(): return lax.ppermute(block, axis, route)  40.1 us
    ppermute x8, starting transfers between devices, passed_along(): return lax.ppermute(block, axis, route)  19.9 us
    psum x1, waiting for transfers between devices, axis_by_axis(): inner = lax.psum(value, axis_one)  14.2 us
    dot_general x1, matrix products, body(): jnp.einsum('kij,kjv->iv', tiles, sources.astype(jnp.bfloat16), preferred_...  10.2 us
    dot_general x1, local copies, waits for them, and re-layouts, body(): jnp.einsum('kw,wrv->krv', picker, stacked, preferred_element_type=jnp.flo...  9.05 us
    dot_general x1, matrix products, body(): jnp.einsum('kw,wrv->krv', picker, stacked, preferred_element_type=jnp.flo...  8.67 us
    unnamed x22, local copies, waits for them, and re-layouts  6.05 us
  transfers between devices with their start and end apart: 10, of which 4 were waited for; matrix products, arithmetic and copies ran while one was open for 11% of the time, Pallas kernels for 0%

profile of v1, /device:TPU:0, one launch (start us, length us, event | category | flops | bytes accessed | tf_op | source)
XLA Modules:
  0.0 240.5 jit_solution(8750324200065911623)
XLA Ops:
  8.1 1.7 convolution_convert_fusion
  9.9 1.0 convolution_bitcast_fusion.1
  10.9 0.9 broadcast_multiply_fusion
  11.9 1.3 bitcast_multiply_fusion.1
  13.2 5.9 %collective-permute-start = (bf16[768,512]{1,0:T(8,128)(2,1)S(1)}, bf16[768,512]{1,0:T(8,128)(2,1)}, u32[]{:S(2)}, u32[]{:S(2)}) collective-permute-start(bf16[768,512]{1,0:T(8,128)(2,1)S(1)} %bitcast_multiply_fusion.1), channel_id=1, source_target_pairs={{0,8},{2,10},{4,12},{6,14},{8,16},{10,18},{12,20},{14,22},{16,24},... | collective-permute-start | bytes 2359304 | tf_op jit(solution)/shard_map/ppermute | solution.py:17
  19.1 3.5 %collective-permute-start.1 = (bf16[768,512]{1,0:T(8,128)(2,1)S(1)}, bf16[768,512]{1,0:T(8,128)(2,1)}, u32[]{:S(2)}, u32[]{:S(2)}) collective-permute-start(bf16[768,512]{1,0:T(8,128)(2,1)S(1)} %bitcast_multiply_fusion.1), channel_id=1, source_target_pairs={{0,6},{2,8},{4,10},{6,12},{8,14},{10,16},{12,18},{14,20},{16,22},{... | collective-permute-start | bytes 2359304 | tf_op jit(solution)/shard_map/ppermute | solution.py:17
  22.6 3.4 %collective-permute-start.2 = (bf16[768,512]{1,0:T(8,128)(2,1)S(1)}, bf16[768,512]{1,0:T(8,128)(2,1)}, u32[]{:S(2)}, u32[]{:S(2)}) collective-permute-start(bf16[768,512]{1,0:T(8,128)(2,1)S(1)} %bitcast_multiply_fusion.1), channel_id=1, source_target_pairs={{0,4},{2,6},{4,8},{6,10},{8,12},{10,14},{12,16},{14,18},{16,20},{1... | collective-permute-start | bytes 2359304 | tf_op jit(solution)/shard_map/ppermute | solution.py:17
  26.0 1.8 collective-permute-start.3
  27.8 1.3 collective-permute-start.4
  29.2 14.2 %all-reduce.3.cloned.1.call-done = f32[2,128,512]{2,1,0:T(8,128)} async-done(((f32[2,128,512]{2,1,0:T(8,128)}), f32[2,128,512]{2,1,0:T(8,128)}) %all-reduce.3.cloned.1.call-update) | async-done | bytes 524304 | tf_op jit(solution)/shard_map/psum | solution.py:10
  43.4 99.0 %all-reduce.4 = bf16[2,128,512]{2,1,0:T(8,128)(2,1)} all-reduce(f32[2,128,512]{2,1,0:T(8,128)} %all-reduce.3.cloned.1.call-done), channel_id=1, replica_groups=mesh['leaf'=16,'top'=2] {'leaf'}, use_global_device_ids=true, to_apply=%region_1.0 | all-reduce | flops 131072 | bytes 786432 | tf_op jit(solution)/shard_map/psum | solution.py:11
  142.4 1.4 fusion.18
  143.8 1.1 fusion.11
  144.9 1.3 collective-permute-start.5
  146.2 1.2 bitcast_dynamic-update-slice_fusion.7
  147.4 1.3 collective-permute-start.6
  148.7 1.2 bitcast_dynamic-update-slice_fusion.6
  149.9 1.5 collective-permute-start.7
  151.4 1.2 bitcast_dynamic-update-slice_fusion.5
  152.7 0.2 fusion.15
  153.0 14.3 %collective-permute-done.5 = bf16[768,512]{1,0:T(8,128)(2,1)S(1)} collective-permute-done((bf16[768,512]{1,0:T(8,128)(2,1)S(1)}, bf16[768,512]{1,0:T(8,128)(2,1)S(1)}, u32[]{:S(2)}, u32[]{:S(2)}) %collective-permute-start.5) | collective-permute-done | bytes 786464 | tf_op jit(solution)/shard_map/ppermute | solution.py:17
  167.3 3.5 %collective-permute-done.6 = bf16[768,512]{1,0:T(8,128)(2,1)S(1)} collective-permute-done((bf16[768,512]{1,0:T(8,128)(2,1)S(1)}, bf16[768,512]{1,0:T(8,128)(2,1)S(1)}, u32[]{:S(2)}, u32[]{:S(2)}) %collective-permute-start.6) | collective-permute-done | bytes 786464 | tf_op jit(solution)/shard_map/ppermute | solution.py:17
  170.8 22.4 %collective-permute-done.7 = bf16[768,512]{1,0:T(8,128)(2,1)S(1)} collective-permute-done((bf16[768,512]{1,0:T(8,128)(2,1)S(1)}, bf16[768,512]{1,0:T(8,128)(2,1)S(1)}, u32[]{:S(2)}, u32[]{:S(2)}) %collective-permute-start.7) | collective-permute-done | bytes 786464 | tf_op jit(solution)/shard_map/ppermute | solution.py:17
  193.3 8.7 %fusion = bf16[8,768,512]{2,0,1:T(8,128)(2,1)} fusion(bf16[9,768,512]{2,1,0:T(8,128)(2,1)S(1)} %bitcast_dynamic-update-slice_fusion, s32[9]{0:T(128)S(1)} %iota_add_fusion, s32[8]{0:T(128)S(1)} %bitcast.91), kind=kOutput, calls=%fused_computation | convolution fusion | flops 56623176 | bytes 13369412 | tf_op jit(solution)/shard_map/kw,wrv->krv/dot_general | solution.py:46
  201.9 9.1 %copy.12 = bf16[8,768,512]{1,2,0:T(8,128)(2,1)} copy(bf16[8,768,512]{2,0,1:T(8,128)(2,1)} %fusion) | data formatting | bytes 12582912 | tf_op jit(solution)/shard_map/kw,wrv->krv/dot_general | solution.py:46
  211.0 2.3 copy.17
  213.3 3.6 %copy.13 = bf16[16,128,512]{2,0,1:T(8,128)(2,1)} copy(bf16[16,128,512]{1,0,2:T(8,128)(2,1)S(1)} %bitcast.88) | data formatting | bytes 4194304 | tf_op jit(solution)/shard_map/all_gather | solution.py:71
  216.8 2.1 fusion.29
  218.9 0.6 convolution_bitcast_fusion.2
  219.5 1.7 fusion.13
  221.2 10.2 %fusion.6 = f32[1,1,768,512]{2,3,1,0:T(8,128)S(1)} fusion(f32[512,768]{1,0:T(8,128)} %fusion.13, bf16[1,1,8,768,768]{4,3,2,1,0:T(8,128)(2,1)} %param.10, bf16[8,768,512]{1,2,0:T(8,128)(2,1)} %copy.12, f32[768]{0:T(1024)S(1)} %fusion.37), kind=kOutput, calls=%fused_computation.8 | convolution fusion | flops 4832624640 | bytes 18877440 | tf_op jit(solution)/shard_map/kij,kjv->iv/dot_general | solution.py:47
  231.4 1.6 copy.10
  (34 shorter events, 0.4 us)
Async XLA Ops:
  7.4 211.6 %copy-start = (bf16[1,1,7,128,128]{4,3,2,1,0:T(8,128)(2,1)S(1)}, bf16[1,1,7,128,128]{4,3,2,1,0:T(8,128)(2,1)}, u32[]{:S(2)}) copy-start(bf16[1,1,7,128,128]{4,3,2,1,0:T(8,128)(2,1)} %param.13) | copy-start | bytes 688132
  7.4 145.3 %copy-start.1 = (bf16[1,1,768,512]{3,2,1,0:T(8,128)(2,1)S(1)}, bf16[1,1,768,512]{3,2,1,0:T(8,128)(2,1)}, u32[]{:S(2)}) copy-start(bf16[1,1,768,512]{3,2,1,0:T(8,128)(2,1)} %param.9) | copy-start | bytes 2359300
  7.4 36.0 %all-reduce.3.cloned.1.call-start = ((), (), s32[]{:S(2)}) async-start(), calls=%async_computation | async-start | bytes 1048576 | tf_op jit(solution)/shard_map/psum | solution.py:10
  9.9 19.2 %copy-start.2 = (bf16[512,128]{1,0:T(8,128)(2,1)}, bf16[512,128]{1,0:T(8,128)(2,1)S(1)}, u32[]{:S(2)}) copy-start(bf16[512,128]{1,0:T(8,128)(2,1)S(1)} %convolution_convert_fusion) | copy-start | bytes 393220
  11.9 199.2 %all-gather.3.cloned.1.call-start = ((), (), s32[]{:S(2)}) async-start(), calls=%async_computation.1 | async-start | bytes 2228224 | tf_op jit(solution)/shard_map/all_gather | solution.py:71
  13.2 131.7 %collective-permute-start = (bf16[768,512]{1,0:T(8,128)(2,1)S(1)}, bf16[768,512]{1,0:T(8,128)(2,1)}, u32[]{:S(2)}, u32[]{:S(2)}) collective-permute-start(bf16[768,512]{1,0:T(8,128)(2,1)S(1)} %bitcast_multiply_fusion.1), channel_id=1, source_target_pairs={{0,8},{2,10},{4,12},{6,14},{8,16},{10,18},{12,20},{14,22},{16,24},... | collective-permute-start | bytes 2359304 | tf_op jit(solution)/shard_map/ppermute | solution.py:17
  19.1 128.3 %collective-permute-start.1 = (bf16[768,512]{1,0:T(8,128)(2,1)S(1)}, bf16[768,512]{1,0:T(8,128)(2,1)}, u32[]{:S(2)}, u32[]{:S(2)}) collective-permute-start(bf16[768,512]{1,0:T(8,128)(2,1)S(1)} %bitcast_multiply_fusion.1), channel_id=1, source_target_pairs={{0,6},{2,8},{4,10},{6,12},{8,14},{10,16},{12,18},{14,20},{16,22},{... | collective-permute-start | bytes 2359304 | tf_op jit(solution)/shard_map/ppermute | solution.py:17
  22.6 127.3 %collective-permute-start.2 = (bf16[768,512]{1,0:T(8,128)(2,1)S(1)}, bf16[768,512]{1,0:T(8,128)(2,1)}, u32[]{:S(2)}, u32[]{:S(2)}) collective-permute-start(bf16[768,512]{1,0:T(8,128)(2,1)S(1)} %bitcast_multiply_fusion.1), channel_id=1, source_target_pairs={{0,4},{2,6},{4,8},{6,10},{8,12},{10,14},{12,16},{14,18},{16,20},{1... | collective-permute-start | bytes 2359304 | tf_op jit(solution)/shard_map/ppermute | solution.py:17
  26.0 126.6 %collective-permute-start.3 = (bf16[768,512]{1,0:T(8,128)(2,1)S(1)}, bf16[768,512]{1,0:T(8,128)(2,1)S(1)}, u32[]{:S(2)}, u32[]{:S(2)}) collective-permute-start(bf16[768,512]{1,0:T(8,128)(2,1)S(1)} %bitcast_multiply_fusion.1), channel_id=1, source_target_pairs={{0,2},{2,4},{4,6},{6,8},{8,10},{10,12},{12,14},{14,16},{16,18},{18... | collective-permute-start | bytes 2359304 | tf_op jit(solution)/shard_map/ppermute | solution.py:17
  27.8 125.1 %collective-permute-start.4 = (bf16[768,512]{1,0:T(8,128)(2,1)S(1)}, bf16[768,512]{1,0:T(8,128)(2,1)S(1)}, u32[]{:S(2)}, u32[]{:S(2)}) collective-permute-start(bf16[768,512]{1,0:T(8,128)(2,1)S(1)} %bitcast_multiply_fusion.1), channel_id=1, source_target_pairs={{2,0},{4,2},{6,4},{8,6},{10,8},{12,10},{14,12},{16,14},{18,16},{20... | collective-permute-start | bytes 2359304 | tf_op jit(solution)/shard_map/ppermute | solution.py:17
  144.9 48.3 %copy-start.5 = (s32[1,1,8]{2,1,0:T(1,128)S(1)}, s32[1,1,8]{2,1,0:T(1,128)}, u32[]{:S(2)}) copy-start(s32[1,1,8]{2,1,0:T(1,128)} %param.15) | copy-start | bytes 100
  144.9 22.3 %collective-permute-start.5 = (bf16[768,512]{1,0:T(8,128)(2,1)S(1)}, bf16[768,512]{1,0:T(8,128)(2,1)S(1)}, u32[]{:S(2)}, u32[]{:S(2)}) collective-permute-start(bf16[768,512]{1,0:T(8,128)(2,1)S(1)} %bitcast_multiply_fusion.1), channel_id=1, source_target_pairs={{4,0},{6,2},{8,4},{10,6},{12,8},{14,10},{16,12},{18,14},{20,16},{2... | collective-permute-start | bytes 2359304 | tf_op jit(solution)/shard_map/ppermute | solution.py:17
  147.4 23.3 %collective-permute-start.6 = (bf16[768,512]{1,0:T(8,128)(2,1)S(1)}, bf16[768,512]{1,0:T(8,128)(2,1)S(1)}, u32[]{:S(2)}, u32[]{:S(2)}) collective-permute-start(bf16[768,512]{1,0:T(8,128)(2,1)S(1)} %bitcast_multiply_fusion.1), channel_id=1, source_target_pairs={{6,0},{8,2},{10,4},{12,6},{14,8},{16,10},{18,12},{20,14},{22,16},{... | collective-permute-start | bytes 2359304 | tf_op jit(solution)/shard_map/ppermute | solution.py:17
  149.9 43.3 %collective-permute-start.7 = (bf16[768,512]{1,0:T(8,128)(2,1)S(1)}, bf16[768,512]{1,0:T(8,128)(2,1)S(1)}, u32[]{:S(2)}, u32[]{:S(2)}) collective-permute-start(bf16[768,512]{1,0:T(8,128)(2,1)S(1)} %bitcast_multiply_fusion.1), channel_id=1, source_target_pairs={{8,0},{10,2},{12,4},{14,6},{16,8},{18,10},{20,12},{22,14},{24,16},... | collective-permute-start | bytes 2359304 | tf_op jit(solution)/shard_map/ppermute | solution.py:17
  211.0 5.9 %copy-start.6 = (s32[1,1,7]{2,1,0:T(1,128)S(1)}, s32[1,1,7]{2,1,0:T(1,128)}, u32[]{:S(2)}) copy-start(s32[1,1,7]{2,1,0:T(1,128)} %param.16) | copy-start | bytes 88
  211.0 8.5 %copy-start.3 = (bf16[1,1,768,128]{3,2,1,0:T(8,128)(2,1)S(1)}, bf16[1,1,768,128]{3,2,1,0:T(8,128)(2,1)}, u32[]{:S(2)}) copy-start(bf16[1,1,768,128]{3,2,1,0:T(8,128)(2,1)} %param.11) | copy-start | bytes 589828
  211.0 8.5 %copy-start.4 = (bf16[1,1,128,128]{3,2,1,0:T(8,128)(2,1)S(1)}, bf16[1,1,128,128]{3,2,1,0:T(8,128)(2,1)}, u32[]{:S(2)}) copy-start(bf16[1,1,128,128]{3,2,1,0:T(8,128)(2,1)} %param.12) | copy-start | bytes 98308
Sparse Core Ops, SparseCore 0:
  12.0 31.3 all-reduce.2
Sparse Core Ops, SparseCore 1:
  29.2 51.8 all-gather.2
